TPU v7x, 128 devices: a whole 4x4x4 slice. The times are simulated.
128 devices in a mesh: blk: 16 (over x, z), order: 8 (over y, core).
Axes of the slice: x: 4, y: 4, z: 4, core: 2. Of those that a mesh axis runs over, the one named last changes fastest.
Arguments:
- field: float32 [16, 1024, 4096], P(None, 'blk', 'order'), may hold values from -6 to 6
- ocean_mask: int32 [1024, 4096], P('blk', 'order'), may hold values from 0 to 1, as said below
- plan: int32 [1024], replicated, may hold values from 0 to 768, as said below
- legendre: bfloat16 [768, 1024, 1024], P('blk', 'order'), may hold values from -0.3125 to 0.3125
Outputs:
- coefficients: float32 [1024, 16, 2, 1024], P('blk', None, None, 'order')
Inputs may be any that keep to these rules, and one draw needn't show every extreme that they name: `ocean_mask`: exactly 256 cycles are all land, at the ends of the cycle order; every other cycle has an ocean point. plan is 768 exactly at the cycles that are all land, and names every slot below 768 once at the other cycles; slot p belongs to index p // 48 of blk; the cycles of one index of blk name at most 4 slots of one index, and in every draw some index of blk names exactly 4 slots of some index.
All inputs are finite; a program needn't handle non-finite values.
Results may differ from a plain program's by a relative error of at most 0.0029.
Values may be sent and summed in bfloat16 or wider, within the bound.
A program may use at most 128 MiB of HBM per device.

v0:
```python
import math
import jax
import jax.numpy as jnp
from jax import lax
from jax.sharding import PartitionSpec as P

NLON = 4096
M = 1024


def twiddle(first, count):
    longitudes = first + jnp.arange(count, dtype=jnp.int32)
    orders = jnp.arange(M, dtype=jnp.int32)
    product = longitudes[:, None] * orders[None, :] % NLON
    angle = product.astype(jnp.float32) * (2.0 * math.pi / NLON)
    scale = 1.0 / math.sqrt(NLON)
    return jnp.stack([jnp.cos(angle) * scale, -jnp.sin(angle) * scale], axis=1)


def transform(values, table):
    return jnp.einsum("frn,ncm->frcm", values, table, precision=lax.Precision.HIGHEST)


def pack_cycles(masked, plan, slot_dev):
    n_blk = lax.axis_size("blk")
    own_index = lax.axis_index("blk")
    cycle_dev = masked.shape[1]
    cap = (cycle_dev + n_blk - 1) // n_blk
    grid = plan.reshape(n_blk, cycle_dev)
    owner = grid // slot_dev
    positions = jnp.arange(cycle_dev, dtype=jnp.int32)
    earlier = positions[None, :] < positions[:, None]
    same_owner = owner[:, :, None] == owner[:, None, :]
    rank = jnp.sum(same_owner & earlier[None], axis=2, dtype=jnp.int32)
    send_pos = owner * cap + rank
    local_pos = lax.dynamic_index_in_dim(send_pos, own_index, 0, keepdims=False)
    buffer_ids = jnp.arange(n_blk * cap, dtype=jnp.int32)
    send_onehot = (buffer_ids[:, None] == local_pos[None, :]).astype(jnp.float32)
    outgoing = jnp.einsum("qr,frn->fqn", send_onehot, masked, precision=lax.Precision.HIGHEST)
    arrived = lax.all_to_all(outgoing, "blk", split_axis=1, concat_axis=1, tiled=True)
    source_pos = (jnp.arange(n_blk, dtype=jnp.int32)[:, None] * cap + rank).reshape(-1)
    mine = (owner == own_index).reshape(-1)
    slot_local = (grid % slot_dev).reshape(-1)
    slot_ids = jnp.arange(slot_dev, dtype=jnp.int32)
    slot_onehot = ((slot_local[None, :] == slot_ids[:, None]) & mine[None, :]).astype(jnp.float32)
    source_onehot = (source_pos[:, None] == buffer_ids[None, :]).astype(jnp.float32)
    receive_map = jnp.dot(slot_onehot, source_onehot, precision=lax.Precision.HIGHEST)
    return jnp.einsum("pq,fqn->fpn", receive_map, arrived, precision=lax.Precision.HIGHEST)


def body(field, ocean_mask, plan, legendre):
    lon_local = field.shape[2]
    slot_dev = legendre.shape[0]
    masked = field * ocean_mask.astype(jnp.float32)[None]
    packed = pack_cycles(masked, plan, slot_dev)
    first = lax.axis_index("order") * lon_local
    terms = transform(packed, twiddle(first, lon_local))
    spectrum = lax.psum_scatter(terms, "order", scatter_dimension=3, tiled=True).astype(
        jnp.bfloat16
    )
    terms = jnp.einsum("pml,fpcm->lfcm", legendre, spectrum, preferred_element_type=jnp.float32)
    coefficients = lax.psum_scatter(terms, "blk", scatter_dimension=0, tiled=True)
    return coefficients


def solution(mesh):
    placed = (P(None, "blk", "order"), P("blk", "order"), P(), P("blk", "order", None))
    return jax.shard_map(
        body, mesh=mesh, in_specs=placed, out_specs=P("blk", None, None, "order"), check_vma=False
    )
```

profile of v0, /device:TPU:1, one launch (start us, length us, event | category | flops | bytes accessed | tf_op | source)
XLA Modules:
  0.0 278.1 jit_solution(17178055627215693072)
XLA Ops:
  6.6 0.7 add_select_fusion.3
  7.3 0.7 fusion.31
  8.0 0.1 and.67
  8.0 0.1 div.20
  8.1 0.9 convert_element_type.26
  9.0 0.5 convert_reduce_fusion
  9.6 3.0 %fusion.18 = f32[16,64,512]{2,1,0:T(8,128)S(1)} fusion(f32[16,64,512]{2,1,0:T(8,128)} %param.4, f32[64,512]{1,0:T(8,128)S(1)} %convert_element_type.26, s32[64]{0:T(128)S(1)} %fusion.33), kind=kOutput, calls=%fused_computation.22 | convolution fusion | flops 403181568 | bytes 4325632 | tf_op jit(solution)/shard_map/qr,frn->fqn/dot_general | solution.py:39
  12.6 2.5 copy.10
  15.1 8.4 %all-to-all-start = ((f32[16,64,512]{2,0,1:T(8,128)}), f32[16,64,512]{2,0,1:T(8,128)S(1)}, u32[]{:S(2)}, u32[]{:S(2)}) async-start(f32[16,64,512]{2,0,1:T(8,128)} %copy.10), calls=%async_computation | async-start | bytes 4194304 | tf_op jit(solution)/shard_map/all_to_all | solution.py:40
  23.6 0.1 broadcast_add_fusion
  23.7 0.1 add.77
  23.8 0.3 convolution_bitcast_fusion
  24.1 10.8 %cosine_multiply_fusion = (f32[512,1,1024]{2,0,1:T(8,128)}, f32[512,1,1024]{2,0,1:T(8,128)}) fusion(s32[512]{0:T(512)S(1)} %iota_add_fusion), kind=kLoop, calls=%fused_computation.16 | loop fusion | flops 8912896 | bytes 4196352 | tf_op jit(solution)/shard_map/mul | solution.py:17
  34.8 16.8 %all-to-all-done = f32[16,64,512]{2,0,1:T(8,128)S(1)} async-done(((f32[16,64,512]{2,0,1:T(8,128)}), f32[16,64,512]{2,0,1:T(8,128)S(1)}, u32[]{:S(2)}, u32[]{:S(2)}) %all-to-all-start) | async-done | bytes 2097184 | tf_op jit(solution)/shard_map/all_to_all | solution.py:40
  51.7 2.9 %fusion.11 = f32[16,512,48]{1,2,0:T(8,128)S(1)} fusion(f32[48,64,1]{1,0,2:T(8,128)S(1)} %convolution_bitcast_fusion, f32[16,64,512]{2,0,1:T(8,128)S(1)} %all-to-all-done), kind=kOutput, calls=%fused_computation.13 | convolution fusion | flops 301989888 | bytes 3682304 | tf_op jit(solution)/shard_map/pq,fqn->fpn/dot_general | solution.py:48
  54.6 13.4 %fusion.5 = f32[16,48,2,1024]{3,1,2,0:T(8,128)} fusion(f32[512,1,1024]{2,0,1:T(8,128)} %get-tuple-element.10, f32[512,1,1024]{2,0,1:T(8,128)S(1)} %copy-done, f32[16,512,48]{1,2,0:T(8,128)S(1)} %fusion.11), kind=kOutput, calls=%fused_computation.4 | convolution fusion | flops 9664724992 | bytes 12058624 | tf_op jit(solution)/shard_map/frn,ncm->frcm/dot_general | solution.py:21
  68.0 0.2 reduce-scatter.5.cloned.1.call-start
  68.3 42.5 %reduce-scatter.3.cloned.1.call-done = f32[16,48,2,128]{3,1,2,0:T(8,128)} async-done(((f32[16,48,2,1024]{3,1,2,0:T(8,128)}), f32[16,48,2,128]{3,1,2,0:T(8,128)}) %reduce-scatter.3.cloned.1.call-update) | async-done | bytes 786448 | tf_op jit(solution)/shard_map/reduce_scatter | solution.py:58
  110.8 1.2 convert_element_type.29
  112.0 1.4 copy.12
  113.4 26.5 %fusion.2 = f32[1024,16,2,128]{0,1,2,3:T(8,128)} fusion(bf16[16,48,2,128]{1,0,2,3:T(8,128)(2,1)S(1)} %copy.12, bf16[48,128,1024,1]{2,1,0,3:T(8,128)(2,1)} %bitcast.24), kind=kOutput, calls=%fused_computation.2 | convolution fusion | flops 402653184 | bytes 29753344 | tf_op jit(solution)/shard_map/pml,fpcm->lfcm/dot_general | solution.py:61
  139.9 17.5 %copy.14 = f32[1024,16,2,128]{3,1,2,0:T(8,128)} copy(f32[1024,16,2,128]{0,1,2,3:T(8,128)} %fusion.2) | data formatting | bytes 33554432 | tf_op jit(solution)/shard_map/pml,fpcm->lfcm/transpose | solution.py:61
  157.4 111.1 %reduce-scatter.5.cloned.1.call-done = f32[64,16,2,128]{3,1,2,0:T(8,128)} async-done(((f32[1024,16,2,128]{3,1,2,0:T(8,128)}), f32[64,16,2,128]{3,1,2,0:T(8,128)}) %reduce-scatter.5.cloned.1.call-update) | async-done | bytes 1048592 | tf_op jit(solution)/shard_map/reduce_scatter | solution.py:62
  268.5 2.7 copy.15
  (10 shorter events, 0.1 us)
Async XLA Ops:
  15.1 36.6 %all-to-all-start = ((f32[16,64,512]{2,0,1:T(8,128)}), f32[16,64,512]{2,0,1:T(8,128)S(1)}, u32[]{:S(2)}, u32[]{:S(2)}) async-start(f32[16,64,512]{2,0,1:T(8,128)} %copy.10), calls=%async_computation | async-start | bytes 4194304 | tf_op jit(solution)/shard_map/all_to_all | solution.py:40
  23.5 87.2 %reduce-scatter.3.cloned.1.call-start = ((), (), s32[]{:S(2)}) async-start(), calls=%async_computation.3 | async-start | bytes 7077888 | tf_op jit(solution)/shard_map/reduce_scatter | solution.py:58
  51.7 3.0 %copy-start = (f32[512,1,1024]{2,0,1:T(8,128)S(1)}, f32[512,1,1024]{2,0,1:T(8,128)}, u32[]{:S(2)}) copy-start(f32[512,1,1024]{2,0,1:T(8,128)} %get-tuple-element.9) | copy-start | bytes 6291460
  68.0 200.5 %reduce-scatter.5.cloned.1.call-start = ((), (), s32[]{:S(2)}) async-start(), calls=%async_computation.4 | async-start | bytes 17825792 | tf_op jit(solution)/shard_map/reduce_scatter | solution.py:62
Sparse Core Ops, SparseCore 0:
  68.1 42.5 reduce-scatter.2
  157.5 110.9 reduce-scatter.4
where the time goes:
time: 279 us; the launch traced here: 278 us
  waiting for transfers between devices  170 us (61%)
  matrix products  46.1 us (17%)
  local copies, waits for them, and re-layouts  24.4 us (9%)
  other arithmetic  14.9 us (5%)
  between operations  13.5 us (5%)
  starting transfers between devices  8.68 us (3%)
    reduce_scatter x1, waiting for transfers between devices, body(): lax.psum_scatter(terms, 'blk', scatter_dimension=0, tiled=True)  111 us
    reduce_scatter x1, waiting for transfers between devices, body(): lax.psum_scatter(terms, 'order', scatter_dimension=3, tiled=True)  42.5 us
    dot_general x1, matrix products, body(): jnp.einsum('pml,fpcm->lfcm', legendre, spectrum, preferred_element_type=j...  26.5 us
    transpose x1, local copies, waits for them, and re-layouts, body(): jnp.einsum('pml,fpcm->lfcm', legendre, spectrum, preferred_element_type=j...  17.5 us
    all_to_all x1, waiting for transfers between devices, pack_cycles(): lax.all_to_all(outgoing, 'blk', split_axis=1, concat_axis=1, tiled=True)  16.8 us
    dot_general x1, matrix products, transform(): jnp.einsum('frn,ncm->frcm', values, table, precision=lax.Precision.HIGHEST)  13.4 us
    mul x1, other arithmetic, twiddle(): return jnp.stack([jnp.cos(angle) * scale, -jnp.sin(angle) * scale], axis=1)  10.8 us
    all_to_all x1, starting transfers between devices, pack_cycles(): lax.all_to_all(outgoing, 'blk', split_axis=1, concat_axis=1, tiled=True)  8.42 us
  transfers between devices with their start and end apart: 3, of which 3 were waited for; matrix products, arithmetic and copies ran while one was open for 4% of the time, Pallas kernels for 0%

commit v1 on v0

--- a/solution.py
+++ b/solution.py
@@ -37,7 +37,10 @@
     buffer_ids = jnp.arange(n_blk * cap, dtype=jnp.int32)
     send_onehot = (buffer_ids[:, None] == local_pos[None, :]).astype(jnp.float32)
     outgoing = jnp.einsum("qr,frn->fqn", send_onehot, masked, precision=lax.Precision.HIGHEST)
-    arrived = lax.all_to_all(outgoing, "blk", split_axis=1, concat_axis=1, tiled=True)
+    arrived = jnp.concatenate(
+        lax.all_to_all(jnp.stack(jnp.split(outgoing, lax.axis_size("blk"), axis=1)), "blk", 0, 0),
+        axis=1,
+    )
     source_pos = (jnp.arange(n_blk, dtype=jnp.int32)[:, None] * cap + rank).reshape(-1)
     mine = (owner == own_index).reshape(-1)
     slot_local = (grid % slot_dev).reshape(-1)

time: 279 us -> 287 us (1.029)
  local copies, waits for them, and re-layouts: 24.4 us -> 33.5 us
    unnamed x2 -> x19, local copies, waits for them, and re-layouts: 0.01 us -> 10.2 us
where the time goes in v1:
time: 287 us; the launch traced here: 286 us
  waiting for transfers between devices  170 us (59%)
  matrix products  44.9 us (16%)
  local copies, waits for them, and re-layouts  33.5 us (12%)
  other arithmetic  14.8 us (5%)
  between operations  13.5 us (5%)
  starting transfers between devices  8.9 us (3%)
    reduce_scatter x1, waiting for transfers between devices, body(): lax.psum_scatter(terms, 'blk', scatter_dimension=0, tiled=True)  111 us
    reduce_scatter x1, waiting for transfers between devices, body(): lax.psum_scatter(terms, 'order', scatter_dimension=3, tiled=True)  42.5 us
    dot_general x1, matrix products, body(): jnp.einsum('pml,fpcm->lfcm', legendre, spectrum, preferred_element_type=j...  26.5 us
    transpose x1, local copies, waits for them, and re-layouts, body(): jnp.einsum('pml,fpcm->lfcm', legendre, spectrum, preferred_element_type=j...  17.5 us
    all_to_all x1, waiting for transfers between devices, pack_cycles(): lax.all_to_all(jnp.stack(jnp.split(outgoing, lax.axis_size('blk'), axis=1...  16.7 us
    dot_general x1, matrix products, transform(): jnp.einsum('frn,ncm->frcm', values, table, precision=lax.Precision.HIGHEST)  12.1 us
    mul x1, other arithmetic, twiddle(): return jnp.stack([jnp.cos(angle) * scale, -jnp.sin(angle) * scale], axis=1)  10.7 us
    unnamed x19, local copies, waits for them, and re-layouts  10.2 us
  transfers between devices with their start and end apart: 3, of which 3 were waited for; matrix products, arithmetic and copies ran while one was open for 4% of the time, Pallas kernels for 0%

profile of v1, /device:TPU:1, one launch (start us, length us, event | category | flops | bytes accessed | tf_op | source)
XLA Modules:
  0.0 285.9 jit_solution(7186310194876344481)
XLA Ops:
  6.6 0.7 add_select_fusion.3
  7.3 0.7 fusion.47
  8.1 0.9 convert_element_type.26
  9.6 3.0 %fusion.18 = f32[16,64,512]{2,1,0:T(8,128)S(1)} fusion(f32[16,64,512]{2,1,0:T(8,128)} %param.4, f32[64,512]{1,0:T(8,128)S(1)} %convert_element_type.26, s32[64]{0:T(128)S(1)} %fusion.49), kind=kOutput, calls=%fused_computation.22 | convolution fusion | flops 403181568 | bytes 4325632 | tf_op jit(solution)/shard_map/qr,frn->fqn/dot_general | solution.py:39
  14.6 0.7 fusion.38
  15.9 0.7 fusion.36
  16.6 0.7 fusion.35
  17.3 0.7 fusion.34
  20.0 0.7 fusion.30
  20.7 0.7 fusion.29
  22.1 0.7 fusion.27
  22.8 0.7 fusion.26
  23.5 8.4 %all-to-all-start = ((f32[16,16,4,512]{3,2,1,0:T(4,128)}), f32[16,16,4,512]{3,2,1,0:T(4,128)S(1)}, u32[]{:S(2)}, u32[]{:S(2)}) async-start(f32[16,16,4,512]{3,2,1,0:T(4,128)} %fusion.26), calls=%async_computation | async-start | bytes 4194304 | tf_op jit(solution)/shard_map/all_to_all | solution.py:41
  32.6 10.7 %cosine_multiply_fusion = (f32[512,1,1024]{2,0,1:T(8,128)}, f32[512,1,1024]{2,0,1:T(8,128)}) fusion(s32[512]{0:T(512)S(1)} %iota_add_fusion), kind=kLoop, calls=%fused_computation.16 | loop fusion | flops 8912896 | bytes 4196352 | tf_op jit(solution)/shard_map/mul | solution.py:17
  43.3 16.7 %all-to-all-done = f32[16,16,4,512]{3,2,1,0:T(4,128)S(1)} async-done(((f32[16,16,4,512]{3,2,1,0:T(4,128)}), f32[16,16,4,512]{3,2,1,0:T(4,128)S(1)}, u32[]{:S(2)}, u32[]{:S(2)}) %all-to-all-start) | async-done | bytes 2097184 | tf_op jit(solution)/shard_map/all_to_all | solution.py:41
  60.7 2.9 %fusion.11 = f32[16,512,48]{1,2,0:T(8,128)S(1)} fusion(f32[48,64,1]{1,0,2:T(8,128)S(1)} %convolution_bitcast_fusion, f32[16,64,512]{2,0,1:T(8,128)S(1)} %bitcast.91), kind=kOutput, calls=%fused_computation.13 | convolution fusion | flops 301989888 | bytes 3682304 | tf_op jit(solution)/shard_map/pq,fqn->fpn/dot_general | solution.py:51
  63.7 12.1 %fusion.5 = f32[16,48,2,1024]{3,1,2,0:T(8,128)} fusion(f32[512,1,1024]{2,0,1:T(8,128)S(1)} %copy-done.1, f32[512,1,1024]{2,0,1:T(8,128)S(1)} %copy-done, f32[16,512,48]{1,2,0:T(8,128)S(1)} %fusion.11), kind=kOutput, calls=%fused_computation.4 | convolution fusion | flops 9664724992 | bytes 12058624 | tf_op jit(solution)/shard_map/frn,ncm->frcm/dot_general | solution.py:21
  76.1 42.5 %reduce-scatter.3.cloned.1.call-done = f32[16,48,2,128]{3,1,2,0:T(8,128)} async-done(((f32[16,48,2,1024]{3,1,2,0:T(8,128)}), f32[16,48,2,128]{3,1,2,0:T(8,128)}) %reduce-scatter.3.cloned.1.call-update) | async-done | bytes 786448 | tf_op jit(solution)/shard_map/reduce_scatter | solution.py:61
  118.6 1.2 convert_element_type.29
  119.8 1.4 copy.18
  121.2 26.5 %fusion.2 = f32[1024,16,2,128]{0,1,2,3:T(8,128)} fusion(bf16[16,48,2,128]{1,0,2,3:T(8,128)(2,1)S(1)} %copy.18, bf16[48,128,1024,1]{2,1,0,3:T(8,128)(2,1)} %bitcast.90), kind=kOutput, calls=%fused_computation.2 | convolution fusion | flops 402653184 | bytes 29753344 | tf_op jit(solution)/shard_map/pml,fpcm->lfcm/dot_general | solution.py:64
  147.7 17.5 %copy.20 = f32[1024,16,2,128]{3,1,2,0:T(8,128)} copy(f32[1024,16,2,128]{0,1,2,3:T(8,128)} %fusion.2) | data formatting | bytes 33554432 | tf_op jit(solution)/shard_map/pml,fpcm->lfcm/transpose | solution.py:64
  165.3 111.0 %reduce-scatter.5.cloned.1.call-done = f32[64,16,2,128]{3,1,2,0:T(8,128)} async-done(((f32[1024,16,2,128]{3,1,2,0:T(8,128)}), f32[64,16,2,128]{3,1,2,0:T(8,128)}) %reduce-scatter.5.cloned.1.call-update) | async-done | bytes 1048592 | tf_op jit(solution)/shard_map/reduce_scatter | solution.py:65
  276.3 2.7 copy.21
  (28 shorter events, 7.7 us)
Async XLA Ops:
  23.5 36.6 %all-to-all-start = ((f32[16,16,4,512]{3,2,1,0:T(4,128)}), f32[16,16,4,512]{3,2,1,0:T(4,128)S(1)}, u32[]{:S(2)}, u32[]{:S(2)}) async-start(f32[16,16,4,512]{3,2,1,0:T(4,128)} %fusion.26), calls=%async_computation | async-start | bytes 4194304 | tf_op jit(solution)/shard_map/all_to_all | solution.py:41
  31.9 86.7 %reduce-scatter.3.cloned.1.call-start = ((), (), s32[]{:S(2)}) async-start(), calls=%async_computation.3 | async-start | bytes 7077888 | tf_op jit(solution)/shard_map/reduce_scatter | solution.py:61
  60.0 3.6 %copy-start.1 = (f32[512,1,1024]{2,0,1:T(8,128)S(1)}, f32[512,1,1024]{2,0,1:T(8,128)}, u32[]{:S(2)}) copy-start(f32[512,1,1024]{2,0,1:T(8,128)} %get-tuple-element.10) | copy-start | bytes 6291460
  60.7 3.0 %copy-start = (f32[512,1,1024]{2,0,1:T(8,128)S(1)}, f32[512,1,1024]{2,0,1:T(8,128)}, u32[]{:S(2)}) copy-start(f32[512,1,1024]{2,0,1:T(8,128)} %get-tuple-element.9) | copy-start | bytes 6291460
  75.9 200.5 %reduce-scatter.5.cloned.1.call-start = ((), (), s32[]{:S(2)}) async-start(), calls=%async_computation.4 | async-start | bytes 17825792 | tf_op jit(solution)/shard_map/reduce_scatter | solution.py:65
Sparse Core Ops, SparseCore 0:
  76.0 42.5 reduce-scatter.2
  165.4 110.8 reduce-scatter.4
